TPU v7x, 64 devices: a 2x2x8 block of a 4x4x8 slice. The times are simulated.
64 devices in a mesh: dp: 4 (over x, y), vp: 16 (over z, core).
Axes of the slice: x: 2, y: 2, z: 8, core: 2. Of those that a mesh axis runs over, the one named last changes fastest.
The devices are a block of a 4x4x8 slice.
Arguments:
- hidden: bfloat16 [4096, 8192], P('dp'), parts along dimension 0
- w_head: bfloat16 [8192, 32000], P(None, 'vp')
- inv_temp: float32 [4096], P('dp'), parts along dimension 0
- target: int32 [4096], P('dp'), parts along dimension 0
Outputs:
- output 1: float32 [4096, 32000], P('dp', 'vp'), parts along dimension 0
- output 2: float32 [4096], P('dp'), parts along dimension 0
There are 4 independent parts. A program takes and returns all parts, laid end to end along the dimension named above; an argument that names none is the same for every part.
All inputs are finite; a program needn't handle non-finite values.
Results may differ from a plain program's by a relative error of at most 0.001.
Values are sent between devices in bfloat16 or wider.
A program may use at most 768 MiB of HBM per device.

v0:
```python
import jax
import jax.numpy as jnp
from jax import lax
from jax.sharding import PartitionSpec as P, NamedSharding


def solution(mesh):
    def local_fn(h_rows, w_cols, tau_rows, tgt_rows):
        shard_width = w_cols.shape[1]
        shard_idx = lax.axis_index("vp")
        logits = jnp.dot(h_rows, w_cols, preferred_element_type=jnp.float32) * tau_rows[:, None]
        local_max = jnp.max(logits, axis=1)
        run_sum = jnp.cumsum(jnp.exp(logits - local_max[:, None]), axis=1)
        pair_stats = jnp.stack([local_max, run_sum[:, -1]])
        all_stats = lax.all_gather(pair_stats, "vp")
        all_maxes = all_stats[:, 0]
        all_sums = all_stats[:, 1]
        glob_max = jnp.max(all_maxes, axis=0)
        scaled = all_sums * jnp.exp(all_maxes - glob_max[None, :])
        glob_sum = jnp.sum(scaled, axis=0)
        before = (jnp.arange(all_stats.shape[0]) < shard_idx)[:, None]
        offset = jnp.sum(jnp.where(before, scaled, 0.0), axis=0)
        cdf_local = (run_sum * jnp.exp(local_max - glob_max)[:, None] + offset[:, None]) / glob_sum[:, None]
        local_pos = tgt_rows - shard_idx * shard_width
        inside = (local_pos >= 0) & (local_pos < shard_width)
        picked = jnp.take_along_axis(cdf_local, jnp.clip(local_pos, 0, shard_width - 1)[:, None], axis=1)[:, 0]
        cdf_target = lax.psum(jnp.where(inside, picked, 0.0), "vp")
        return cdf_local, cdf_target

    return jax.shard_map(
        local_fn,
        mesh=mesh,
        in_specs=(P("dp", None), P(None, "vp"), P("dp"), P("dp")),
        out_specs=(P("dp", "vp"), P("dp")),
        check_vma=False,
    )
```

profile of v0, /device:TPU:21, one launch (start us, length us, event | category | flops | bytes accessed | tf_op | source)
XLA Modules:
  0.0 178.3 jit_solution(4109816179759058460)
XLA Ops:
  0.6 0.0 copy-start.2
  0.6 45.2 %multiply_reduce_fusion = (f32[1024]{0:T(1024)S(1)}, f32[1024,2000]{0,1:T(8,128)S(1)}) fusion(f32[1024]{0:T(1024)} %param.6, bf16[1024,8192]{1,0:T(8,128)(2,1)} %param.4, bf16[8192,2000]{0,1:T(8,128)(2,1)} %param.5), kind=kOutput, calls=%fused_computation.7 | convolution fusion | flops 33558528000 | bytes 57745408 | tf_op jit(solution)/shard_map/dot_general | solution.py:11
  45.8 0.0 copy-done.2
  45.8 2.0 %subtract_exponential_fusion = f32[1024,2000]{0,1:T(8,128)S(1)} fusion(f32[1024,2000]{0,1:T(8,128)S(1)} %get-tuple-element.8, f32[1024]{0:T(1024)S(1)} %get-tuple-element.7, f32[1024]{0:T(1024)S(1)} %copy-done.2), kind=kLoop, calls=%fused_computation.6 | loop fusion | flops 4096000 | bytes 16392192 | tf_op jit(solution)/shard_map/exp | solution.py:13
  47.8 4.3 %pad.3 = f32[1024,2048]{0,1:T(8,128)} pad(f32[1024,2000]{0,1:T(8,128)S(1)} %subtract_exponential_fusion, f32[]{:T(128)} %constant.11.clone.1), padding=0_0x0_48 | pad | bytes 16580612 | tf_op jit(solution)/shard_map/pad
  52.1 11.4 %fusion = f32[1024,16,128]{0,1,2:T(8,128)} fusion(f32[1024,16,128]{0,2,1:T(8,128)} %bitcast.34), kind=kOutput, calls=%fused_computation.1 | output fusion | flops 266338304 | bytes 16777216 | tf_op jit(solution)/shard_map/reduce-window
  63.5 0.8 slice_bitcast_fusion
  64.4 0.1 reduce-window.9
  64.5 4.4 %broadcast_add_fusion = f32[1024,16,128]{0,1,2:T(8,128)S(1)} fusion(f32[1024,16,128]{0,1,2:T(8,128)} %fusion, f32[1024,16]{0,1:T(8,128)S(1)} %slice.28), kind=kLoop, calls=%fused_computation.8 | loop fusion | flops 2097152 | bytes 16842752 | tf_op jit(solution)/shard_map/reduce_window_sum
  68.8 5.1 %copy.12 = f32[1024,16,128]{0,2,1:T(8,128)S(1)} copy(f32[1024,16,128]{0,1,2:T(8,128)S(1)} %broadcast_add_fusion) | data formatting | bytes 16777216 | tf_op jit(solution)/shard_map/reduce_window_sum
  73.9 0.0 copy-start
  73.9 3.2 %copy-done = f32[1024,16,128]{0,2,1:T(8,128)} copy-done((f32[1024,16,128]{0,2,1:T(8,128)}, f32[1024,16,128]{0,2,1:T(8,128)S(1)}, u32[]{:S(2)}) %copy-start) | copy-done | bytes 8388632
  77.2 23.1 %all-gather.1 = f32[16,2,1024]{2,1,0:T(2,128)S(1)} all-gather(f32[1,2,1024]{2,1,0:T(2,128)S(1)} %maximum_bitcast_fusion), channel_id=2, replica_groups=mesh['dp'=4,'vp'=16] {'vp'}, dimensions={0}, use_global_device_ids=true | all-gather | bytes 139264 | tf_op jit(solution)/shard_map/all_gather | solution.py:15
  100.2 0.0 copy-start.1
  100.2 0.1 fusion.10
  100.4 0.1 select_reduce_fusion
  100.5 8.6 %fusion.3 = f32[1024,2000]{0,1:T(8,128)} fusion(f32[1024,2048]{0,1:T(8,128)} %bitcast.36, f32[1024]{0:T(1024)S(1)} %get-tuple-element.3, f32[1024]{0:T(1024)S(1)} %get-tuple-element.2, f32[1024]{0:T(1024)S(1)} %subtract_exponential_fusion.1), kind=kLoop, calls=%fused_computation.5 | loop fusion | flops 6144000 | bytes 16396288 | tf_op jit(solution)/shard_map/div | solution.py:23
  109.1 0.0 copy-done.1
  109.2 45.4 %gather_fusion = f32[1024]{0:T(1024)S(1)} fusion(f32[1024,2000]{0,1:T(8,128)} %fusion.3, s32[1024]{0:T(1024)S(1)} %bitcast.33), kind=kCustom, calls=%fused_computation | custom fusion | bytes 16384 | tf_op jit(solution)/shard_map/jit(take_along_axis)/gather | solution.py:26
  154.6 23.7 %psum.7 = f32[1024]{0:T(1024)} all-reduce(f32[1024]{0:T(1024)S(1)} %select_select_fusion), channel_id=1, replica_groups=mesh['dp'=4,'vp'=16] {'vp'}, use_global_device_ids=true, to_apply=%region_6.7 | all-reduce | flops 1024 | bytes 8192 | tf_op jit(solution)/shard_map/psum | solution.py:27
  (10 shorter events, 0.1 us)
Async XLA Ops:
  0.6 45.2 %copy-start.2 = (f32[1024]{0:T(1024)S(1)}, f32[1024]{0:T(1024)}, u32[]{:S(2)}) copy-start(f32[1024]{0:T(1024)} %param.6) | copy-start | bytes 12292
  73.9 3.2 %copy-start = (f32[1024,16,128]{0,2,1:T(8,128)}, f32[1024,16,128]{0,2,1:T(8,128)S(1)}, u32[]{:S(2)}) copy-start(f32[1024,16,128]{0,2,1:T(8,128)S(1)} %copy.12) | copy-start | bytes 25165828
  100.2 8.9 %copy-start.1 = (s32[1024]{0:T(1024)S(1)}, s32[1024]{0:T(1024)}, u32[]{:S(2)}) copy-start(s32[1024]{0:T(1024)} %param.7) | copy-start | bytes 12292
where the time goes:
time: 179 us; the launch traced here: 178 us
  local copies, waits for them, and re-layouts  58.8 us (33%)
  blocking collectives  46.8 us (26%)
  matrix products  45.2 us (25%)
  other arithmetic  26.8 us (15%)
    gather x1, local copies, waits for them, and re-layouts, local_fn(): jnp.take_along_axis(cdf_local, jnp.clip(local_pos, 0, shard_width - 1)[:,...  45.4 us
    dot_general x1, matrix products, local_fn(): jnp.dot(h_rows, w_cols, preferred_element_type=jnp.float32)  45.2 us
    psum x1, blocking collectives, local_fn(): cdf_target = lax.psum(jnp.where(inside, picked, 0.0), 'vp')  23.7 us
    all_gather x1, blocking collectives, local_fn(): all_stats = lax.all_gather(pair_stats, 'vp')  23.1 us
    another operation x3, other arithmetic  15.9 us
    div x1, other arithmetic, local_fn(): (run_sum * jnp.exp(local_max - glob_max)[:, None] + offset[:, None]) / gl...  8.65 us
    another operation x3, local copies, waits for them, and re-layouts  5.93 us
    pad x1, local copies, waits for them, and re-layouts  4.29 us

commit v1 on v0

v1 whole, which is shorter than its diff:
```python
import functools

import jax
import jax.numpy as jnp
from jax import lax
from jax.experimental import pallas as pl
from jax.experimental.pallas import tpu as pltpu
from jax.sharding import PartitionSpec as P

LANES = 128
SUB = 8
TILE = 400
FOLD = 10
UNIT = 512
DEPTH = 1024
AHEAD = 2
F32 = jnp.float32
NT = (((1,), (1,)), ((), ()))


def head_kernel(n_dev, h_hbm, w_hbm, tau_ref, tgt_ref, sums_ref, gain_ref, off_ref, tsum_ref,
                w_ref, ha_ref, hb_ref, stat_ref, snd, rcv,
                w_sem, ha_sem, hb_sem, send_sem, recv_sem):
    width, depth = w_hbm.shape
    n_k = depth // DEPTH
    per_unit = UNIT // LANES
    n_tile = width // TILE
    me = lax.axis_index("vp")

    barrier = pltpu.get_barrier_semaphore()

    @pl.loop(1, n_dev)
    def _(d):
        pl.semaphore_signal(barrier, inc=1, device_id={"vp": lax.rem(me + d, n_dev)},
                            device_id_type=pl.DeviceIdType.MESH)

    def w_copy(k):
        ks = pl.ds(pl.multiple_of(k * DEPTH, DEPTH), DEPTH)
        return pltpu.make_async_copy(w_hbm.at[:, ks], w_ref.at[:, ks], w_sem.at[k])

    def ha_copy(k):
        slot = lax.rem(k, AHEAD)
        ks = pl.ds(pl.multiple_of(k * DEPTH, DEPTH), DEPTH)
        return pltpu.make_async_copy(h_hbm.at[pl.ds(0, UNIT), ks], ha_ref.at[slot], ha_sem.at[slot])

    def hb_copy():
        return pltpu.make_async_copy(h_hbm.at[pl.ds(UNIT, UNIT), :], hb_ref, hb_sem.at[0])

    for k in range(AHEAD):
        w_copy(k).start()
        ha_copy(k).start()

    sums_ref[0:per_unit] = jnp.zeros((per_unit, width, LANES), F32)
    first = me * width
    shape = (TILE // SUB, SUB, LANES)
    sub = lax.broadcasted_iota(jnp.int32, shape, 1)
    token = lax.broadcasted_iota(jnp.int32, shape, 0) * SUB + sub

    def finish(g, t, z):
        n = TILE // SUB
        z = (z * tau_ref[g:g + 1, :]).reshape(shape)
        top = jnp.max(jnp.max(z, axis=0), axis=0, keepdims=True)
        p = jnp.exp(z - top[None])
        local = tgt_ref[g:g + 1, :] - (first + t * TILE)
        upto = jnp.sum(jnp.where(token <= local[None], p, 0.0), axis=0)
        stat_ref[g, t:t + 1, :] = top
        stat_ref[g, 2 * n_tile + t:2 * n_tile + t + 1, :] = jnp.sum(upto, axis=0, keepdims=True)
        for s in (1, 2, 4):
            p = p + jnp.where(sub >= s, pltpu.roll(p, s, 1), 0.0)
        last = jnp.broadcast_to(p[:, SUB - 1:, :], shape).reshape(n // FOLD, FOLD, SUB, LANES)
        p = p.reshape(n // FOLD, FOLD, SUB, LANES)
        run = last[:, 0]
        cols = [p[:, 0]]
        for i in range(1, FOLD):
            cols.append(p[:, i] + run)
            run = run + last[:, i]
        ahead = jnp.zeros((1, SUB, LANES), F32)
        starts = []
        for i in range(n // FOLD):
            starts.append(ahead)
            ahead = ahead + run[i:i + 1]
        p = jnp.stack(cols, axis=1) + jnp.concatenate(starts, axis=0)[:, None]
        sums_ref[g, t * TILE:(t + 1) * TILE, :] = p.reshape(TILE, LANES)
        stat_ref[g, n_tile + t:n_tile + t + 1, :] = ahead[0, 0:1, :]

    def finish_step(u, t, z):
        for j in range(per_unit):
            finish(u * per_unit + j, t, z[:, j * LANES:(j + 1) * LANES])

    def peer_copy(u, d):
        peer = lax.rem(me + d, n_dev)
        return pltpu.make_async_remote_copy(
            src_ref=snd.at[u], dst_ref=rcv.at[u, me], send_sem=send_sem.at[u, peer],
            recv_sem=recv_sem.at[u, me], device_id={"vp": peer}, device_id_type=pl.DeviceIdType.MESH)

    def send_unit(u):
        for j in range(per_unit):
            g = u * per_unit + j
            top_t = stat_ref[g, 0:n_tile, :]
            top = jnp.max(top_t, axis=0, keepdims=True)
            e = jnp.exp(top_t - top)
            s = jnp.sum(e * stat_ref[g, n_tile:2 * n_tile, :], axis=0, keepdims=True)
            t = jnp.sum(e * stat_ref[g, 2 * n_tile:3 * n_tile, :], axis=0, keepdims=True)
            for i, x in enumerate((top, s, t)):
                snd[u, i, j:j + 1, :] = x
                rcv[u, me, i, j:j + 1, :] = x

        @pl.loop(1, n_dev)
        def _(d):
            peer_copy(u, d).start()

    def receive_unit(u):
        @pl.loop(1, n_dev)
        def _(d):
            src = lax.rem(me + d, n_dev)
            pltpu.make_async_remote_copy(
                src_ref=snd.at[u], dst_ref=rcv.at[u, src], send_sem=send_sem.at[u, src],
                recv_sem=recv_sem.at[u, src], device_id={"vp": src},
                device_id_type=pl.DeviceIdType.MESH).wait()

        tops = rcv[u, :, 0]
        peak = jnp.max(tops, axis=0)
        e = jnp.exp(tops - peak[None])
        part = rcv[u, :, 1] * e
        total = jnp.sum(part, axis=0)
        device = lax.broadcasted_iota(jnp.int32, part.shape, 0)
        before = jnp.sum(jnp.where(device < me, part, 0.0), axis=0)
        upto = jnp.sum(rcv[u, :, 2] * e, axis=0)
        inv = 1.0 / total
        tsum_ref[u * per_unit:(u + 1) * per_unit, :] = upto * inv
        for j in range(per_unit):
            g = u * per_unit + j
            a_t = jnp.exp(stat_ref[g, 0:n_tile, :] - peak[j:j + 1, :])
            s_t = stat_ref[g, n_tile:2 * n_tile, :] * a_t
            gain_ref[g] = a_t * inv[j:j + 1, :]
            run = before[j:j + 1, :]
            for t in range(n_tile):
                off_ref[g, t:t + 1, :] = run * inv[j:j + 1, :]
                run = run + s_t[t:t + 1, :]

    def first_rows(k, last):
        w_copy(k).wait()
        ha_copy(k).wait()
        slot = lax.rem(k, AHEAD)
        ks = pl.ds(pl.multiple_of(k * DEPTH, DEPTH), DEPTH)
        for t in range(n_tile):
            ts = slice(t * TILE, (t + 1) * TILE)
            z = lax.dot_general(w_ref[ts, ks], ha_ref[slot], NT, preferred_element_type=F32)
            for j in range(per_unit):
                part = sums_ref[j, ts, :] + z[:, j * LANES:(j + 1) * LANES]
                if last:
                    finish(j, t, part)
                else:
                    sums_ref[j, ts, :] = part

    @pl.loop(0, n_k - 1)
    def _(k):
        first_rows(k, False)

        @pl.when(k + AHEAD < n_k)
        def _():
            w_copy(k + AHEAD).start()
            ha_copy(k + AHEAD).start()

        @pl.when(k + AHEAD == n_k)
        def _():
            hb_copy().start()

    first_rows(n_k - 1, True)
    pl.semaphore_wait(barrier, n_dev - 1)
    send_unit(0)

    hb_copy().wait()
    for t in range(n_tile):
        z = lax.dot_general(w_ref[t * TILE:(t + 1) * TILE, :], hb_ref[...], NT, preferred_element_type=F32)
        finish_step(1, t, z)
    send_unit(1)

    for u in range(2):
        receive_unit(u)


def write_kernel(sums_ref, gain_ref, off_ref, tsum_ref, out_hbm, tgt_out, stage, sem):
    groups, width, _ = sums_ref.shape
    slots, chunk = stage.shape[0], stage.shape[1]
    tgt_out[...] = tsum_ref[...]
    n = width // chunk

    def out_copy(i):
        return pltpu.make_async_copy(stage.at[i % slots], out_hbm.at[pl.ds(i * chunk, chunk), :], sem.at[i % slots])

    for i in range(n):
        if i >= slots:
            out_copy(i - slots).wait()
        rs = slice(i * chunk, (i + 1) * chunk)
        t = i * chunk // TILE
        for g in range(groups):
            stage[i % slots, :, g * LANES:(g + 1) * LANES] = (
                sums_ref[g, rs, :] * gain_ref[g, t:t + 1, :] + off_ref[g, t:t + 1, :])
        out_copy(i).start()
    for i in range(max(0, n - slots), n):
        out_copy(i).wait()


def solution(mesh):
    n_dev = mesh.shape["vp"]

    def local_fn(h_rows, w_cols, tau_rows, tgt_rows):
        rows, depth = h_rows.shape
        width = w_cols.shape[1]
        groups = rows // LANES
        n_unit = rows // UNIT
        n_k = depth // DEPTH
        n_tile = width // TILE
        per_unit = UNIT // LANES
        vmem = pl.BlockSpec(memory_space=pltpu.VMEM)
        hbm = pl.BlockSpec(memory_space=pltpu.HBM)
        sums, gain, off, tsum = pl.pallas_call(
            functools.partial(head_kernel, n_dev),
            out_shape=(
                jax.ShapeDtypeStruct((groups, width, LANES), F32),
                jax.ShapeDtypeStruct((groups, n_tile, LANES), F32),
                jax.ShapeDtypeStruct((groups, n_tile, LANES), F32),
                jax.ShapeDtypeStruct((groups, LANES), F32),
            ),
            in_specs=[hbm, hbm, vmem, vmem],
            out_specs=(vmem, vmem, vmem, vmem),
            scratch_shapes=[
                pltpu.VMEM((width, depth), jnp.bfloat16),
                pltpu.VMEM((AHEAD, UNIT, DEPTH), jnp.bfloat16),
                pltpu.VMEM((UNIT, depth), jnp.bfloat16),
                pltpu.VMEM((groups, 3 * n_tile, LANES), F32),
                pltpu.VMEM((n_unit, 3, per_unit, LANES), F32),
                pltpu.VMEM((n_unit, n_dev, 3, per_unit, LANES), F32),
                pltpu.SemaphoreType.DMA((n_k,)),
                pltpu.SemaphoreType.DMA((AHEAD,)),
                pltpu.SemaphoreType.DMA((1,)),
                pltpu.SemaphoreType.DMA((n_unit, n_dev)),
                pltpu.SemaphoreType.DMA((n_unit, n_dev)),
            ],
            compiler_params=pltpu.CompilerParams(
                collective_id=0, has_side_effects=True, vmem_limit_bytes=44 * 2**20),
            name="head",
        )(h_rows, w_cols.T, tau_rows.reshape(groups, LANES), tgt_rows.reshape(groups, LANES))
        table, picked = pl.pallas_call(
            write_kernel,
            out_shape=(
                jax.ShapeDtypeStruct((width, rows), F32),
                jax.ShapeDtypeStruct((groups, LANES), F32),
            ),
            in_specs=[vmem, vmem, vmem, vmem],
            out_specs=(hbm, vmem),
            scratch_shapes=[
                pltpu.VMEM((4, TILE // 2, rows), F32),
                pltpu.SemaphoreType.DMA((4,)),
            ],
            compiler_params=pltpu.CompilerParams(vmem_limit_bytes=16 * 2**20),
            name="write",
        )(sums, gain, off, tsum)
        return table.T, picked.reshape(rows)

    return jax.shard_map(
        local_fn,
        mesh=mesh,
        in_specs=(P("dp", None), P(None, "vp"), P("dp"), P("dp")),
        out_specs=(P("dp", "vp"), P("dp")),
        check_vma=False,
    )
```

time: 179 us -> 65.2 us (0.36)
  Pallas kernels: 0 us -> 62.9 us
  local copies, waits for them, and re-layouts: 58.8 us -> 1.37 us
  blocking collectives: 46.8 us -> 0 us
  matrix products: 45.2 us -> 0 us
  other arithmetic: 26.8 us -> 0 us
    pallas_call x0 -> x2, Pallas kernels: none -> 62.9 us  [the longest x1 58.9 us: local_fn(): pl.pallas_call(functools.partial(head_kernel, n_dev), out_shape=(jax.Shap...]
    gather x1 -> x0, local copies, waits for them, and re-layouts: 45.4 us -> none  [local_fn(): jnp.take_along_axis(cdf_local, jnp.clip(local_pos, 0, shard_width - 1)[:,...]
    dot_general x1 -> x0, matrix products: 45.2 us -> none  [local_fn(): jnp.dot(h_rows, w_cols, preferred_element_type=jnp.float32)]
    psum x1 -> x0, blocking collectives: 23.7 us -> none  [local_fn(): cdf_target = lax.psum(jnp.where(inside, picked, 0.0), 'vp')]
    all_gather x1 -> x0, blocking collectives: 23.1 us -> none  [local_fn(): all_stats = lax.all_gather(pair_stats, 'vp')]
    another operation x3 -> x0, other arithmetic: 15.9 us -> none
    div x1 -> x0, other arithmetic: 8.65 us -> none  [local_fn(): (run_sum * jnp.exp(local_max - glob_max)[:, None] + offset[:, None]) / gl...]
    another operation x4 -> x0, local copies, waits for them, and re-layouts: 5.93 us -> none
where the time goes in v1:
time: 65.2 us; the launch traced here: 65.1 us
  Pallas kernels  62.9 us (96%)
  local copies, waits for them, and re-layouts  1.37 us (2%)
  between operations  0.83 us (1%)
    pallas_call x1, Pallas kernels, local_fn(): pl.pallas_call(functools.partial(head_kernel, n_dev), out_shape=(jax.Shap...  58.9 us
    pallas_call x1, Pallas kernels, local_fn(): pl.pallas_call(write_kernel, out_shape=(jax.ShapeDtypeStruct((width, rows...  3.98 us
    unnamed x4, local copies, waits for them, and re-layouts  1.37 us

profile of v1, /device:TPU:21, one launch (start us, length us, event | category | flops | bytes accessed | tf_op | source)
XLA Modules:
  0.0 65.1 jit_solution(13962042786852447024)
XLA Ops:
  0.6 0.0 copy-start
  0.6 0.7 %copy-done = f32[1024]{0:T(1024)S(1)} copy-done((f32[1024]{0:T(1024)S(1)}, f32[1024]{0:T(1024)}, u32[]{:S(2)}) %copy-start) | copy-done | bytes 4120
  1.3 0.0 copy-start.1
  1.3 0.7 %copy-done.1 = s32[1024]{0:T(1024)S(1)} copy-done((s32[1024]{0:T(1024)S(1)}, s32[1024]{0:T(1024)}, u32[]{:S(2)}) %copy-start.1) | copy-done | bytes 4120
  2.0 58.9 %head.1 = (f32[8,2000,128]{2,1,0:T(8,128)S(1)}, f32[8,5,128]{2,1,0:T(8,128)S(1)}, f32[8,5,128]{2,1,0:T(8,128)S(1)}, f32[8,128]{1,0:T(8,128)S(1)}) custom-call(bf16[1024,8192]{1,0:T(8,128)(2,1)} %h_hbm.1, bf16[2000,8192]{1,0:T(8,128)(2,1)} %bitcast.7, f32[8,128]{1,0:T(8,128)S(1)} %bitcast.5, s32[8,128]{1,0:T(8,128)S(1)} %bitcast.6), custom_call_target="tpu_custom_call" | custom-call | tf_op jit(solution)/shard_map/head/pallas_call | solution.py:218
  60.9 4.0 %write.1 = (f32[2000,1024]{1,0:T(8,128)}, f32[8,128]{1,0:T(8,128)}) custom-call(f32[8,2000,128]{2,1,0:T(8,128)S(1)} %get-tuple-element.8.sums_ref, f32[8,5,128]{2,1,0:T(8,128)S(1)} %get-tuple-element.9.gain_ref, f32[8,5,128]{2,1,0:T(8,128)S(1)} %get-tuple-element.10.off_ref, f32[8,128]{1,0:T(8,128)S(1)} %get-tuple-element.11.tsum_ref), custom_call_target="tpu_custom_call" | custom-call | tf_op jit(solution)/shard_map/write/pallas_call | solution.py:245
Async XLA Ops:
  0.6 0.7 %copy-start = (f32[1024]{0:T(1024)S(1)}, f32[1024]{0:T(1024)}, u32[]{:S(2)}) copy-start(f32[1024]{0:T(1024)} %param.6) | copy-start | bytes 12292
  1.3 0.7 %copy-start.1 = (s32[1024]{0:T(1024)S(1)}, s32[1024]{0:T(1024)}, u32[]{:S(2)}) copy-start(s32[1024]{0:T(1024)} %param.7) | copy-start | bytes 12292

commit v2 on v0

v2 whole, which is shorter than its diff:
```python
import functools

import jax
import jax.numpy as jnp
from jax import lax
from jax.experimental import pallas as pl
from jax.experimental.pallas import tpu as pltpu
from jax.sharding import PartitionSpec as P

LANES = 128
SUB = 8
TILE = 80
BLOCK = 400
WIDE = 512
NARROW = 256
DEPTH = 1024
LEAD = (256, 256, 512, 512, 512)
SPREAD = 4
F32 = jnp.float32
NT = (((1,), (1,)), ((), ()))


def head_kernel(n_dev, h_hbm, w_hbm, tau_hbm, tgt_hbm, sums_ref, gain_ref, off_ref, tsum_ref,
                w_ref, h_ref, tau_ref, tgt_ref, top_ref, sum_ref, upto_ref, ltop_ref,
                snd0, snd1, rcv0, rcv1, w_sem, h_sem, in_sem, send_sem, recv_sem):
    width, depth = w_hbm.shape
    rows = h_hbm.shape[0]
    n_chunk = depth // DEPTH
    n_tile = width // TILE
    n_block = width // BLOCK
    units = [(0, WIDE), (WIDE, WIDE)]
    snd = (snd0, snd1)
    rcv = (rcv0, rcv1)
    me = lax.axis_index("vp")

    starts = []
    at = 0
    for size in LEAD:
        starts.append((at, size))
        at += size
    lead_end = at
    while at < depth:
        starts.append((at, DEPTH))
        at += DEPTH

    def copies(i, at, size):
        ks = pl.ds(at, size)
        slot = at // DEPTH
        return (pltpu.make_async_copy(h_hbm.at[pl.ds(0, WIDE), ks],
                                      h_ref.at[slot, :, pl.ds(at - slot * DEPTH, size)], h_sem.at[i]),
                pltpu.make_async_copy(w_hbm.at[:, ks], w_ref.at[:, ks], w_sem.at[i]))

    def late_copy(c):
        ks = pl.ds(pl.multiple_of(c * DEPTH, DEPTH), DEPTH)
        return pltpu.make_async_copy(h_hbm.at[pl.ds(WIDE, rows - WIDE), ks],
                                     h_ref.at[lax.rem(c + n_chunk, n_chunk + 1)], h_sem.at[len(starts) + c])

    tau_copy = pltpu.make_async_copy(tau_hbm, tau_ref, in_sem.at[0])
    tgt_copy = pltpu.make_async_copy(tgt_hbm, tgt_ref, in_sem.at[1])
    for i, (at, size) in enumerate(starts):
        for copy in copies(i, at, size):
            copy.start()
        if i == len(LEAD):
            tau_copy.start()
            tgt_copy.start()
    late_copy(0).start()

    barrier = pltpu.get_barrier_semaphore()

    @pl.loop(1, n_dev)
    def _(d):
        pl.semaphore_signal(barrier, inc=1, device_id={"vp": lax.rem(me + d, n_dev)},
                            device_id_type=pl.DeviceIdType.MESH)

    first = me * width

    def stats(t, c0, z):
        cs = slice(c0, c0 + NARROW)
        n = TILE // SUB
        z = (z * tau_ref[0:1, cs]).reshape(n, SUB, NARROW)
        top = jnp.max(jnp.max(z, axis=0), axis=0, keepdims=True)
        p = jnp.exp(z - top[None])
        token = (lax.broadcasted_iota(jnp.int32, (n, SUB, NARROW), 0) * SUB
                 + lax.broadcasted_iota(jnp.int32, (n, SUB, NARROW), 1))
        local = tgt_ref[0:1, cs] - (first + t * TILE)
        upto = jnp.sum(jnp.where(token <= local[None], p, 0.0), axis=0)
        top_ref[t:t + 1, cs] = top
        upto_ref[t:t + 1, cs] = jnp.sum(upto, axis=0, keepdims=True)
        sum_ref[t:t + 1, cs] = jnp.sum(jnp.sum(p, axis=0), axis=0, keepdims=True)
        return p

    def scan(t, c0, p):
        n = TILE // SUB
        sub = lax.broadcasted_iota(jnp.int32, (n, SUB, NARROW), 1)
        for s in (1, 2, 4):
            p = p + jnp.where(sub >= s, pltpu.roll(p, s, 1), 0.0)
        last = jnp.broadcast_to(p[:, SUB - 1:, :], (n, SUB, NARROW))
        run = last[0:1]
        parts = [p[0:1]]
        for i in range(1, n):
            parts.append(p[i:i + 1] + run)
            if i + 1 < n:
                run = run + last[i:i + 1]
        sums_ref[t * TILE:(t + 1) * TILE, c0:c0 + NARROW] = jnp.concatenate(parts, axis=0).reshape(TILE, NARROW)

    def fold(u):
        c0, wide = units[u]
        cs = slice(c0, c0 + wide)
        top = jnp.max(top_ref[:, cs], axis=0, keepdims=True)
        e = jnp.exp(top_ref[:, cs] - top)
        ltop_ref[0:1, cs] = top
        s = jnp.sum(e * sum_ref[:, cs], axis=0, keepdims=True)
        t = jnp.sum(e * upto_ref[:, cs], axis=0, keepdims=True)
        for j in range(wide // LANES):
            js = slice(j * LANES, (j + 1) * LANES)
            for i, x in enumerate((top, s, t)):
                snd[u][i, j:j + 1, :] = x[:, js]
                rcv[u][me, i, j:j + 1, :] = x[:, js]

        @pl.loop(1, n_dev)
        def _(d):
            peer = lax.rem(me + d, n_dev)
            pltpu.make_async_remote_copy(
                src_ref=snd[u], dst_ref=rcv[u].at[me], send_sem=send_sem.at[u, peer],
                recv_sem=recv_sem.at[u, me], device_id={"vp": peer},
                device_id_type=pl.DeviceIdType.MESH).start()

    def local_parts(u):
        c0, wide = units[u]
        cs = slice(c0, c0 + wide)
        e = jnp.exp(top_ref[:, cs] - ltop_ref[0:1, cs])
        gain_ref[:, cs] = e
        s = e * sum_ref[:, cs]
        run = jnp.zeros((1, wide), F32)
        for t in range(n_tile):
            off_ref[t:t + 1, cs] = run
            run = run + s[t:t + 1, :]

    def receive(u):
        c0, wide = units[u]
        per = wide // LANES
        cs = slice(c0, c0 + wide)

        @pl.loop(1, n_dev)
        def _(d):
            src = lax.rem(me + d, n_dev)
            pltpu.make_async_remote_copy(
                src_ref=snd[u], dst_ref=rcv[u].at[src], send_sem=send_sem.at[u, src],
                recv_sem=recv_sem.at[u, src], device_id={"vp": src},
                device_id_type=pl.DeviceIdType.MESH).wait()

        tops = rcv[u][:, 0]
        peak = jnp.max(tops, axis=0)
        e = jnp.exp(tops - peak[None])
        part = rcv[u][:, 1] * e
        device = lax.broadcasted_iota(jnp.int32, part.shape, 0)
        inv = 1.0 / jnp.sum(part, axis=0)
        before = jnp.sum(jnp.where(device < me, part, 0.0), axis=0) * inv
        tsum_ref[c0 // LANES:c0 // LANES + per, :] = jnp.sum(rcv[u][:, 2] * e, axis=0) * inv

        def row(x):
            return jnp.concatenate([x[j:j + 1, :] for j in range(per)], axis=1)

        f = jnp.exp(ltop_ref[0:1, cs] - row(peak)) * row(inv)
        gain_ref[:, cs] = gain_ref[:, cs] * f
        off_ref[:, cs] = off_ref[:, cs] * f + row(before)

    def add_chunk(at, size, slot, inner, init):
        for block in range(n_block):
            ws = slice(block * BLOCK, (block + 1) * BLOCK)
            z = lax.dot_general(w_ref[ws, pl.ds(at, size)], h_ref[slot, :, inner:inner + size], NT,
                                preferred_element_type=F32)
            sums_ref[ws, 0:WIDE] = z if init else sums_ref[ws, 0:WIDE] + z

    for i, (at, size) in enumerate(starts[:len(LEAD)]):
        for copy in copies(i, at, size):
            copy.wait()
        add_chunk(at, size, at // DEPTH, at % DEPTH, i == 0)
        if (at + size) % DEPTH == 0:
            late_copy((at + size) // DEPTH).start()

    lead = lead_end // DEPTH

    @pl.loop(0, (n_chunk - lead) // 2)
    def _(i):
        c = lead + 2 * i
        for b in range(2):
            for copy in copies(len(LEAD) + 2 * i + b, pl.multiple_of((c + b) * DEPTH, DEPTH), DEPTH):
                copy.wait()
        add_chunk(pl.multiple_of(c * DEPTH, DEPTH), DEPTH, c, 0, False)
        late_copy(c + 1).start()
        add_chunk(pl.multiple_of((c + 1) * DEPTH, DEPTH), DEPTH, c + 1, 0, False)

        @pl.when(c + 2 < n_chunk)
        def _():
            late_copy(c + 2).start()

    tau_copy.wait()
    tgt_copy.wait()

    zero = pl.multiple_of(me // n_dev * SUB, SUB)
    for c in range(n_chunk):
        late_copy(c).wait()
    queue = [(t, c0) for t in range(n_tile) for c0 in range(0, WIDE, NARROW)]
    per_block = BLOCK // TILE

    def block_pieces(block):
        return [(block * per_block + i, WIDE + c0) for i in range(per_block) for c0 in range(0, WIDE, NARROW)]

    def raw(t, c0):
        return sums_ref[t * TILE:(t + 1) * TILE, c0:c0 + NARROW]

    done = 0
    for block in range(n_block):
        ws = slice(block * BLOCK, (block + 1) * BLOCK)
        rs = pl.ds(block * BLOCK + zero, BLOCK)
        pieces = block_pieces(block - 1) if block else []
        reach = len(queue) * min(block + 1, SPREAD) // SPREAD
        pieces += queue[done:reach]
        done = reach
        given = 0
        for c in range(n_chunk):
            z = lax.dot_general(w_ref[ws, c * DEPTH:(c + 1) * DEPTH], h_ref[(c + n_chunk) % (n_chunk + 1)], NT,
                                preferred_element_type=F32)
            sums_ref[rs, WIDE:2 * WIDE] = z if c == 0 else sums_ref[rs, WIDE:2 * WIDE] + z
            reach = len(pieces) * (c + 1) // n_chunk
            for t, c0 in pieces[given:reach]:
                scan(t, c0, stats(t, c0, raw(t, c0)))
            given = reach
        if block == SPREAD - 1:
            pl.semaphore_wait(barrier, n_dev - 1)
            fold(0)
            local_parts(0)

    tail = block_pieces(n_block - 1)
    for t, c0 in tail:
        p = stats(t, c0, raw(t, c0))
        sums_ref[t * TILE:(t + 1) * TILE, c0:c0 + NARROW] = p.reshape(TILE, NARROW)
    fold(1)
    for t, c0 in tail:
        scan(t, c0, raw(t, c0).reshape(TILE // SUB, SUB, NARROW))
    local_parts(1)
    for v in range(2):
        receive(v)


def write_kernel(sums_ref, gain_ref, off_ref, tsum_ref, out_hbm, tgt_out, stage, sem):
    width = sums_ref.shape[0]
    n_tile = width // TILE
    tgt_out[...] = tsum_ref[...]

    def out_copy(t):
        ts = slice(t * TILE, (t + 1) * TILE)
        return pltpu.make_async_copy(stage.at[ts, :], out_hbm.at[ts, :], sem.at[t])

    for t in range(n_tile):
        ts = slice(t * TILE, (t + 1) * TILE)
        stage[ts, :] = sums_ref[ts, :] * gain_ref[t:t + 1, :] + off_ref[t:t + 1, :]
        out_copy(t).start()
    for t in range(n_tile):
        out_copy(t).wait()


def solution(mesh):
    n_dev = mesh.shape["vp"]

    def local_fn(h_rows, w_cols, tau_rows, tgt_rows):
        rows, depth = h_rows.shape
        width = w_cols.shape[1]
        groups = rows // LANES
        n_chunk = depth // DEPTH
        n_copy = len(LEAD) + (depth - sum(LEAD)) // DEPTH
        n_tile = width // TILE
        sizes = (WIDE, rows - WIDE)
        vmem = pl.BlockSpec(memory_space=pltpu.VMEM)
        hbm = pl.BlockSpec(memory_space=pltpu.HBM)
        sums, gain, off, tsum = pl.pallas_call(
            functools.partial(head_kernel, n_dev),
            out_shape=(
                jax.ShapeDtypeStruct((width, rows), F32),
                jax.ShapeDtypeStruct((n_tile, rows), F32),
                jax.ShapeDtypeStruct((n_tile, rows), F32),
                jax.ShapeDtypeStruct((groups, LANES), F32),
            ),
            in_specs=[hbm, hbm, hbm, hbm],
            out_specs=(vmem, vmem, vmem, vmem),
            scratch_shapes=[
                pltpu.VMEM((width, depth), jnp.bfloat16),
                pltpu.VMEM((n_chunk + 1, WIDE, DEPTH), jnp.bfloat16),
                pltpu.VMEM((1, rows), F32),
                pltpu.VMEM((1, rows), jnp.int32),
                pltpu.VMEM((n_tile, rows), F32),
                pltpu.VMEM((n_tile, rows), F32),
                pltpu.VMEM((n_tile, rows), F32),
                pltpu.VMEM((1, rows), F32),
                *[pltpu.VMEM((3, s // LANES, LANES), F32) for s in sizes],
                *[pltpu.VMEM((n_dev, 3, s // LANES, LANES), F32) for s in sizes],
                pltpu.SemaphoreType.DMA((n_copy,)),
                pltpu.SemaphoreType.DMA((n_copy + n_chunk,)),
                pltpu.SemaphoreType.DMA((2,)),
                pltpu.SemaphoreType.DMA((2, n_dev)),
                pltpu.SemaphoreType.DMA((2, n_dev)),
            ],
            compiler_params=pltpu.CompilerParams(
                collective_id=0, has_side_effects=True, vmem_limit_bytes=45 * 2**20),
            name="head",
        )(*[pltpu.with_memory_space_constraint(x, pltpu.HBM)
            for x in (h_rows, w_cols.T, tau_rows.reshape(1, rows), tgt_rows.reshape(1, rows))])
        table, picked = pl.pallas_call(
            write_kernel,
            out_shape=(
                jax.ShapeDtypeStruct((width, rows), F32),
                jax.ShapeDtypeStruct((groups, LANES), F32),
            ),
            in_specs=[vmem, vmem, vmem, vmem],
            out_specs=(hbm, vmem),
            scratch_shapes=[
                pltpu.VMEM((width, rows), F32),
                pltpu.SemaphoreType.DMA((n_tile,)),
            ],
            compiler_params=pltpu.CompilerParams(vmem_limit_bytes=16 * 2**20),
            name="write",
        )(sums, gain, off, tsum)
        return table.T, picked.reshape(rows)

    return jax.shard_map(
        local_fn,
        mesh=mesh,
        in_specs=(P("dp", None), P(None, "vp"), P("dp"), P("dp")),
        out_specs=(P("dp", "vp"), P("dp")),
        check_vma=False,
    )
```

time: 179 us -> 63 us (0.35)
  Pallas kernels: 0 us -> 62.1 us
  local copies, waits for them, and re-layouts: 58.8 us -> 0 us
  blocking collectives: 46.8 us -> 0 us
  matrix products: 45.2 us -> 0 us
  other arithmetic: 26.8 us -> 0 us
    pallas_call x0 -> x2, Pallas kernels: none -> 62.1 us  [the longest x1 58 us: local_fn(): pl.pallas_call(functools.partial(head_kernel, n_dev), out_shape=(jax.Shap...]
    gather x1 -> x0, local copies, waits for them, and re-layouts: 45.4 us -> none  [local_fn(): jnp.take_along_axis(cdf_local, jnp.clip(local_pos, 0, shard_width - 1)[:,...]
    dot_general x1 -> x0, matrix products: 45.2 us -> none  [local_fn(): jnp.dot(h_rows, w_cols, preferred_element_type=jnp.float32)]
    psum x1 -> x0, blocking collectives: 23.7 us -> none  [local_fn(): cdf_target = lax.psum(jnp.where(inside, picked, 0.0), 'vp')]
    all_gather x1 -> x0, blocking collectives: 23.1 us -> none  [local_fn(): all_stats = lax.all_gather(pair_stats, 'vp')]
    another operation x3 -> x0, other arithmetic: 15.9 us -> none
    div x1 -> x0, other arithmetic: 8.65 us -> none  [local_fn(): (run_sum * jnp.exp(local_max - glob_max)[:, None] + offset[:, None]) / gl...]
    another operation x4 -> x0, local copies, waits for them, and re-layouts: 5.93 us -> none
where the time goes in v2:
time: 63 us; the launch traced here: 62.9 us
  Pallas kernels  62.1 us (99%)
  between operations  0.82 us (1%)
    pallas_call x1, Pallas kernels, local_fn(): pl.pallas_call(functools.partial(head_kernel, n_dev), out_shape=(jax.Shap...  58 us
    pallas_call x1, Pallas kernels, local_fn(): pl.pallas_call(write_kernel, out_shape=(jax.ShapeDtypeStruct((width, rows...  4.05 us

profile of v2, /device:TPU:21, one launch (start us, length us, event | category | flops | bytes accessed | tf_op | source)
XLA Modules:
  0.0 62.9 jit_solution(3044721232890699185)
XLA Ops:
  0.6 58.0 %head.1 = (f32[2000,1024]{1,0:T(8,128)S(1)}, f32[25,1024]{1,0:T(8,128)S(1)}, f32[25,1024]{1,0:T(8,128)S(1)}, f32[8,128]{1,0:T(8,128)S(1)}) custom-call(bf16[1024,8192]{1,0:T(8,128)(2,1)} %h_hbm.1, bf16[2000,8192]{1,0:T(8,128)(2,1)} %bitcast.5, f32[1,1024]{1,0:T(1,128)} %bitcast.6, s32[1,1024]{1,0:T(1,128)} %bitcast.7), custom_call_target="tpu_custom_call" | custom-call | tf_op jit(solution)/shard_map/head/pallas_call | solution.py:277
  58.6 4.1 %write.1 = (f32[2000,1024]{1,0:T(8,128)}, f32[8,128]{1,0:T(8,128)}) custom-call(f32[2000,1024]{1,0:T(8,128)S(1)} %get-tuple-element.8.sums_ref, f32[25,1024]{1,0:T(8,128)S(1)} %get-tuple-element.9.gain_ref, f32[25,1024]{1,0:T(8,128)S(1)} %get-tuple-element.10.off_ref, f32[8,128]{1,0:T(8,128)S(1)} %get-tuple-element.11.tsum_ref), custom_call_target="tpu_custom_call" | custom-call | tf_op jit(solution)/shard_map/write/pallas_call | solution.py:309

commit v3 on v2

v3 whole, which is shorter than its diff:
```python
import functools

import jax
import jax.numpy as jnp
from jax import lax
from jax.experimental import pallas as pl
from jax.experimental.pallas import tpu as pltpu
from jax.sharding import PartitionSpec as P

LANES = 128
SUB = 8
BLOCK = 400
STRIP = 50
WIDE = 512
LOG2E = 1.4426950408889634
DEPTH = 1024
LEAD = (256, 256, 512, 512, 512)
PARTS = 5
F32 = jnp.float32
NT = (((1,), (1,)), ((), ()))


def head_kernel(n_dev, h_hbm, w_hbm, tau_hbm, tgt_hbm, sums_ref, gain_ref, off_ref, tsum_ref,
                w_ref, h_ref, tau_ref, tgt_ref, top_ref, sum_ref, upto_ref, ltop_ref,
                snd0, snd1, rcv0, rcv1, w_sem, h_sem, in_sem, send_sem, recv_sem):
    width, depth = w_hbm.shape
    rows = h_hbm.shape[0]
    n_chunk = depth // DEPTH
    per = WIDE // LANES
    n_block = width // BLOCK
    units = [(0, WIDE), (WIDE, WIDE)]
    snd = (snd0, snd1)
    rcv = (rcv0, rcv1)
    me = lax.axis_index("vp")

    starts = []
    at = 0
    for size in LEAD:
        starts.append((at, size))
        at += size
    lead_end = at
    while at < depth:
        starts.append((at, DEPTH))
        at += DEPTH

    def copies(i, at, size):
        ks = pl.ds(at, size)
        slot = at // DEPTH
        return (pltpu.make_async_copy(h_hbm.at[pl.ds(0, WIDE), ks],
                                      h_ref.at[slot, :, pl.ds(at - slot * DEPTH, size)], h_sem.at[i]),
                pltpu.make_async_copy(w_hbm.at[:, ks], w_ref.at[:, ks], w_sem.at[i]))

    def late_copy(c):
        ks = pl.ds(pl.multiple_of(c * DEPTH, DEPTH), DEPTH)
        return pltpu.make_async_copy(h_hbm.at[pl.ds(WIDE, rows - WIDE), ks],
                                     h_ref.at[lax.rem(c + n_chunk, n_chunk + 1)], h_sem.at[len(starts) + c])

    tau_copy = pltpu.make_async_copy(tau_hbm, tau_ref, in_sem.at[0])
    tgt_copy = pltpu.make_async_copy(tgt_hbm, tgt_ref, in_sem.at[1])
    for i, (at, size) in enumerate(starts):
        for copy in copies(i, at, size):
            copy.start()
        if i == len(LEAD):
            tau_copy.start()
            tgt_copy.start()
    late_copy(0).start()

    barrier = pltpu.get_barrier_semaphore()

    @pl.loop(1, n_dev)
    def _(d):
        pl.semaphore_signal(barrier, inc=1, device_id={"vp": lax.rem(me + d, n_dev)},
                            device_id_type=pl.DeviceIdType.MESH)

    first = me * width

    sub = lax.broadcasted_iota(jnp.int32, (per, SUB, LANES), 1)

    def lanes(ref, u):
        return jnp.concatenate([ref[0:1, (u * per + j) * LANES:(u * per + j + 1) * LANES][None] for j in range(per)], axis=0)

    def strip(u, block, i, value=None):
        where = (slice(u * per, (u + 1) * per), pl.ds(block * BLOCK + i, SUB, stride=STRIP), slice(None))
        if value is None:
            return sums_ref[where]
        sums_ref[where] = value

    def strips(u, block, parts):
        cuts = [STRIP * i // parts for i in range(parts + 1)]
        scale = lanes(tau_ref, u) * LOG2E
        top = None
        for lo, hi in zip(cuts, cuts[1:]):
            for i in range(lo, hi):
                z = strip(u, block, i)
                top = z if top is None else jnp.maximum(top, z)
            yield
        top = top * scale
        local = lanes(tgt_ref, u) - (first + block * BLOCK) - sub * STRIP
        run = jnp.zeros((per, SUB, LANES), F32)
        upto = run
        for lo, hi in zip(cuts, cuts[1:]):
            for i in range(lo, hi):
                run = run + jnp.exp2(strip(u, block, i) * scale - top)
                upto = jnp.where(local == i, run, upto)
                strip(u, block, i, run)
            if hi == STRIP:
                top_ref[u, block] = top
                sum_ref[u, block] = run
                upto_ref[u, block] = jnp.where(local >= STRIP, run, upto)
            yield

    def fold(u):
        top = jnp.max(jnp.max(top_ref[u], axis=0), axis=1, keepdims=True)
        e = jnp.exp2(top_ref[u] - top[None])
        ltop_ref[u] = top
        s = jnp.sum(jnp.sum(e * sum_ref[u], axis=0), axis=1, keepdims=True)
        t = jnp.sum(jnp.sum(e * upto_ref[u], axis=0), axis=1, keepdims=True)
        for j in range(per):
            for i, x in enumerate((top, s, t)):
                snd[u][i, j:j + 1, :] = x[j]
                rcv[u][me, i, j:j + 1, :] = x[j]

        @pl.loop(1, n_dev)
        def _(d):
            peer = lax.rem(me + d, n_dev)
            pltpu.make_async_remote_copy(
                src_ref=snd[u], dst_ref=rcv[u].at[me], send_sem=send_sem.at[u, peer],
                recv_sem=recv_sem.at[u, me], device_id={"vp": peer},
                device_id_type=pl.DeviceIdType.MESH).start()

    def local_parts(u):
        run = jnp.zeros((per, 1, LANES), F32)
        for block in range(n_block):
            e = jnp.exp2(top_ref[u, block] - ltop_ref[u])
            gain_ref[block, u * per:(u + 1) * per] = e
            s = e * sum_ref[u, block]
            for k in (1, 2, 4):
                s = s + jnp.where(sub >= k, pltpu.roll(s, k, 1), 0.0)
            off_ref[block, u * per:(u + 1) * per] = jnp.where(sub >= 1, pltpu.roll(s, 1, 1), 0.0) + run
            run = run + s[:, SUB - 1:, :]

    def receive(u):
        @pl.loop(1, n_dev)
        def _(d):
            src = lax.rem(me + d, n_dev)
            pltpu.make_async_remote_copy(
                src_ref=snd[u], dst_ref=rcv[u].at[src], send_sem=send_sem.at[u, src],
                recv_sem=recv_sem.at[u, src], device_id={"vp": src},
                device_id_type=pl.DeviceIdType.MESH).wait()

        tops = rcv[u][:, 0]
        peak = jnp.max(tops, axis=0)
        e = jnp.exp2(tops - peak[None])
        part = rcv[u][:, 1] * e
        device = lax.broadcasted_iota(jnp.int32, part.shape, 0)
        inv = 1.0 / jnp.sum(part, axis=0)
        before = jnp.sum(jnp.where(device < me, part, 0.0), axis=0) * inv
        tsum_ref[u * per:(u + 1) * per, :] = jnp.sum(rcv[u][:, 2] * e, axis=0) * inv

        def spread(x):
            return jnp.concatenate([x[j:j + 1, :][None] for j in range(per)], axis=0)

        f = jnp.exp2(ltop_ref[u] - spread(peak)) * spread(inv)
        before = spread(before)
        us = slice(u * per, (u + 1) * per)
        for block in range(n_block):
            gain_ref[block, us] = gain_ref[block, us] * f
            off_ref[block, us] = off_ref[block, us] * f + before

    def add(u, rs, z, init):
        for j in range(per):
            part = z[:, j * LANES:(j + 1) * LANES]
            sums_ref[u * per + j, rs, :] = part if init else sums_ref[u * per + j, rs, :] + part

    def add_chunk(at, size, slot, inner, init):
        for block in range(n_block):
            ws = slice(block * BLOCK, (block + 1) * BLOCK)
            z = lax.dot_general(w_ref[ws, pl.ds(at, size)], h_ref[slot, :, inner:inner + size], NT,
                                preferred_element_type=F32)
            add(0, ws, z, init)

    for i, (at, size) in enumerate(starts[:len(LEAD)]):
        for copy in copies(i, at, size):
            copy.wait()
        add_chunk(at, size, at // DEPTH, at % DEPTH, i == 0)
        if (at + size) % DEPTH == 0:
            late_copy((at + size) // DEPTH).start()

    lead = lead_end // DEPTH

    @pl.loop(0, (n_chunk - lead) // 2)
    def _(i):
        c = lead + 2 * i
        for b in range(2):
            for copy in copies(len(LEAD) + 2 * i + b, pl.multiple_of((c + b) * DEPTH, DEPTH), DEPTH):
                copy.wait()
        add_chunk(pl.multiple_of(c * DEPTH, DEPTH), DEPTH, c, 0, False)
        late_copy(c + 1).start()
        add_chunk(pl.multiple_of((c + 1) * DEPTH, DEPTH), DEPTH, c + 1, 0, False)

        @pl.when(c + 2 < n_chunk)
        def _():
            late_copy(c + 2).start()

    tau_copy.wait()
    tgt_copy.wait()

    zero = pl.multiple_of(me // n_dev * SUB, SUB)
    for c in range(n_chunk):
        late_copy(c).wait()
    n_step = n_chunk // 2
    first_unit = [strips(0, block, PARTS) for block in range(n_block)]
    for block in range(n_block):
        ws = slice(block * BLOCK, (block + 1) * BLOCK)
        rs = pl.ds(block * BLOCK + zero, BLOCK)
        todo = [strips(1, block - 1, PARTS)] if block else []
        for _ in range(2 if block in (0, 1) else 1 if block == 2 else 0):
            todo.append(first_unit.pop(0))
        turns = [x for x in todo for _ in range(2 * PARTS)]
        given = 0
        for c in range(n_step):
            pair = jnp.concatenate([h_ref[(2 * c + i + n_chunk) % (n_chunk + 1)] for i in range(2)], axis=1)
            z = lax.dot_general(w_ref[ws, 2 * c * DEPTH:2 * (c + 1) * DEPTH], pair, NT, preferred_element_type=F32)
            add(1, rs, z, c == 0)
            reach = len(turns) * (c + 1) // n_step
            for x in turns[given:reach]:
                next(x, None)
            given = reach
        if block == 2:
            pl.semaphore_wait(barrier, n_dev - 1)
            fold(0)
            local_parts(0)

    for _ in strips(1, n_block - 1, 1):
        pass
    fold(1)
    local_parts(1)
    for v in range(2):
        receive(v)


def write_kernel(sums_ref, gain_ref, off_ref, tsum_ref, out_hbm, tgt_out, stage, sem):
    groups, width, _ = sums_ref.shape
    n_block = width // BLOCK
    tgt_out[...] = tsum_ref[...]

    def out_copy(block, g):
        rs = slice(block * BLOCK, (block + 1) * BLOCK)
        return pltpu.make_async_copy(stage.at[g, rs, :], out_hbm.at[rs, g * LANES:(g + 1) * LANES], sem.at[block, g])

    for block in range(n_block):
        for g in range(groups):
            gain = gain_ref[block, g]
            off = off_ref[block, g]
            for i in range(STRIP):
                rows = pl.ds(block * BLOCK + i, SUB, stride=STRIP)
                stage[g, rows, :] = sums_ref[g, rows, :] * gain + off
            out_copy(block, g).start()
    for block in range(n_block):
        for g in range(groups):
            out_copy(block, g).wait()


def solution(mesh):
    n_dev = mesh.shape["vp"]

    def local_fn(h_rows, w_cols, tau_rows, tgt_rows):
        rows, depth = h_rows.shape
        width = w_cols.shape[1]
        groups = rows // LANES
        n_chunk = depth // DEPTH
        n_copy = len(LEAD) + (depth - sum(LEAD)) // DEPTH
        n_block = width // BLOCK
        per = WIDE // LANES
        n_unit = rows // WIDE
        vmem = pl.BlockSpec(memory_space=pltpu.VMEM)
        hbm = pl.BlockSpec(memory_space=pltpu.HBM)
        sums, gain, off, tsum = pl.pallas_call(
            functools.partial(head_kernel, n_dev),
            out_shape=(
                jax.ShapeDtypeStruct((groups, width, LANES), F32),
                jax.ShapeDtypeStruct((n_block, groups, SUB, LANES), F32),
                jax.ShapeDtypeStruct((n_block, groups, SUB, LANES), F32),
                jax.ShapeDtypeStruct((groups, LANES), F32),
            ),
            in_specs=[hbm, hbm, hbm, hbm],
            out_specs=(vmem, vmem, vmem, vmem),
            scratch_shapes=[
                pltpu.VMEM((width, depth), jnp.bfloat16),
                pltpu.VMEM((n_chunk + 1, WIDE, DEPTH), jnp.bfloat16),
                pltpu.VMEM((1, rows), F32),
                pltpu.VMEM((1, rows), jnp.int32),
                *[pltpu.VMEM((n_unit, n_block, per, SUB, LANES), F32) for _ in range(3)],
                pltpu.VMEM((n_unit, per, 1, LANES), F32),
                *[pltpu.VMEM((3, per, LANES), F32) for _ in range(n_unit)],
                *[pltpu.VMEM((n_dev, 3, per, LANES), F32) for _ in range(n_unit)],
                pltpu.SemaphoreType.DMA((n_copy,)),
                pltpu.SemaphoreType.DMA((n_copy + n_chunk,)),
                pltpu.SemaphoreType.DMA((2,)),
                pltpu.SemaphoreType.DMA((2, n_dev)),
                pltpu.SemaphoreType.DMA((2, n_dev)),
            ],
            compiler_params=pltpu.CompilerParams(
                collective_id=0, has_side_effects=True, vmem_limit_bytes=45 * 2**20),
            name="head",
        )(*[pltpu.with_memory_space_constraint(x, pltpu.HBM)
            for x in (h_rows, w_cols.T, tau_rows.reshape(1, rows), tgt_rows.reshape(1, rows))])
        table, picked = pl.pallas_call(
            write_kernel,
            out_shape=(
                jax.ShapeDtypeStruct((width, rows), F32),
                jax.ShapeDtypeStruct((groups, LANES), F32),
            ),
            in_specs=[vmem, vmem, vmem, vmem],
            out_specs=(hbm, vmem),
            scratch_shapes=[
                pltpu.VMEM((groups, width, LANES), F32),
                pltpu.SemaphoreType.DMA((n_block, groups)),
            ],
            compiler_params=pltpu.CompilerParams(vmem_limit_bytes=16 * 2**20),
            name="write",
        )(sums, gain, off, tsum)
        return table.T, picked.reshape(rows)

    return jax.shard_map(
        local_fn,
        mesh=mesh,
        in_specs=(P("dp", None), P(None, "vp"), P("dp"), P("dp")),
        out_specs=(P("dp", "vp"), P("dp")),
        check_vma=False,
    )
```

time: 63 us -> 58.2 us (0.924)
  Pallas kernels: 62.1 us -> 57.3 us
    pallas_call x1, Pallas kernels: 58 us -> 53.1 us  [local_fn(): pl.pallas_call(functools.partial(head_kernel, n_dev), out_shape=(jax.Shap...]
where the time goes in v3:
time: 58.2 us; the launch traced here: 58.1 us
  Pallas kernels  57.3 us (98%)
  between operations  0.82 us (1%)
    pallas_call x1, Pallas kernels, local_fn(): pl.pallas_call(functools.partial(head_kernel, n_dev), out_shape=(jax.Shap...  53.1 us
    pallas_call x1, Pallas kernels, local_fn(): pl.pallas_call(write_kernel, out_shape=(jax.ShapeDtypeStruct((width, rows...  4.18 us

profile of v3, /device:TPU:21, one launch (start us, length us, event | category | flops | bytes accessed | tf_op | source)
XLA Modules:
  0.0 58.1 jit_solution(14380082943097212180)
XLA Ops:
  0.6 53.1 %head.1 = (f32[8,2000,128]{2,1,0:T(8,128)S(1)}, f32[5,8,8,128]{3,2,1,0:T(8,128)S(1)}, f32[5,8,8,128]{3,2,1,0:T(8,128)S(1)}, f32[8,128]{1,0:T(8,128)S(1)}) custom-call(bf16[1024,8192]{1,0:T(8,128)(2,1)} %h_hbm.1, bf16[2000,8192]{1,0:T(8,128)(2,1)} %bitcast.5, f32[1,1024]{1,0:T(1,128)} %bitcast.6, s32[1,1024]{1,0:T(1,128)} %bitcast.7), custom_call_target="tpu_custom_call" | custom-call | tf_op jit(solution)/shard_map/head/pallas_call | solution.py:278
  53.7 4.2 %write.1 = (f32[2000,1024]{1,0:T(8,128)}, f32[8,128]{1,0:T(8,128)}) custom-call(f32[8,2000,128]{2,1,0:T(8,128)S(1)} %get-tuple-element.8.sums_ref, f32[5,8,8,128]{3,2,1,0:T(8,128)S(1)} %get-tuple-element.9.gain_ref, f32[5,8,8,128]{3,2,1,0:T(8,128)S(1)} %get-tuple-element.10.off_ref, f32[8,128]{1,0:T(8,128)S(1)} %get-tuple-element.11.tsum_ref), custom_call_target="tpu_custom_call" | custom-call | tf_op jit(solution)/shard_map/write/pallas_call | solution.py:308

commit v4 on v3

--- a/solution.py
+++ b/solution.py
@@ -229,14 +229,19 @@
         if block == 2:
             pl.semaphore_wait(barrier, n_dev - 1)
             fold(0)
-            local_parts(0)
 
     for _ in strips(1, n_block - 1, 1):
         pass
     fold(1)
+    local_parts(0)
+    receive(0)
     local_parts(1)
-    for v in range(2):
-        receive(v)
+    for block in range(n_block):
+        gain = gain_ref[block, 0:per]
+        off = off_ref[block, 0:per]
+        for i in range(STRIP):
+            strip(0, block, i, strip(0, block, i) * gain + off)
+    receive(1)
 
 
 def write_kernel(sums_ref, gain_ref, off_ref, tsum_ref, out_hbm, tgt_out, stage, sem):
@@ -244,21 +249,28 @@
     n_block = width // BLOCK
     tgt_out[...] = tsum_ref[...]
 
-    def out_copy(block, g):
+    def out_copy(block, g, source, at=None):
         rs = slice(block * BLOCK, (block + 1) * BLOCK)
-        return pltpu.make_async_copy(stage.at[g, rs, :], out_hbm.at[rs, g * LANES:(g + 1) * LANES], sem.at[block, g])
-
-    for block in range(n_block):
-        for g in range(groups):
+        return pltpu.make_async_copy(source.at[g if at is None else at, rs, :], out_hbm.at[rs, g * LANES:(g + 1) * LANES], sem.at[block, g])
+
+    ready = WIDE // LANES
+    for block in range(n_block):
+        for g in range(ready):
+            out_copy(block, g, sums_ref).start()
+    for block in range(n_block):
+        for g in range(ready, groups):
             gain = gain_ref[block, g]
             off = off_ref[block, g]
             for i in range(STRIP):
                 rows = pl.ds(block * BLOCK + i, SUB, stride=STRIP)
-                stage[g, rows, :] = sums_ref[g, rows, :] * gain + off
-            out_copy(block, g).start()
+                stage[g - ready, rows, :] = sums_ref[g, rows, :] * gain + off
+            out_copy(block, g, stage, g - ready).start()
     for block in range(n_block):
         for g in range(groups):
-            out_copy(block, g).wait()
+            if g < ready:
+                out_copy(block, g, sums_ref).wait()
+            else:
+                out_copy(block, g, stage, g - ready).wait()
 
 
 def solution(mesh):
@@ -314,7 +326,7 @@
             in_specs=[vmem, vmem, vmem, vmem],
             out_specs=(hbm, vmem),
             scratch_shapes=[
-                pltpu.VMEM((groups, width, LANES), F32),
+                pltpu.VMEM((groups - per, width, LANES), F32),
                 pltpu.SemaphoreType.DMA((n_block, groups)),
             ],
             compiler_params=pltpu.CompilerParams(vmem_limit_bytes=16 * 2**20),

time: 58.2 us -> 58.1 us (level)
  no operation moved by 1% of the time
where the time goes in v4:
time: 58.1 us; the launch traced here: 58 us
  Pallas kernels  57.2 us (98%)
  between operations  0.82 us (1%)
    pallas_call x1, Pallas kernels, local_fn(): pl.pallas_call(functools.partial(head_kernel, n_dev), out_shape=(jax.Shap...  53 us
    pallas_call x1, Pallas kernels, local_fn(): pl.pallas_call(write_kernel, out_shape=(jax.ShapeDtypeStruct((width, rows...  4.16 us

profile of v4, /device:TPU:21, one launch (start us, length us, event | category | flops | bytes accessed | tf_op | source)
XLA Modules:
  0.0 58.0 jit_solution(9228240546610000322)
XLA Ops:
  0.6 53.0 %head.1 = (f32[8,2000,128]{2,1,0:T(8,128)S(1)}, f32[5,8,8,128]{3,2,1,0:T(8,128)S(1)}, f32[5,8,8,128]{3,2,1,0:T(8,128)S(1)}, f32[8,128]{1,0:T(8,128)S(1)}) custom-call(bf16[1024,8192]{1,0:T(8,128)(2,1)} %h_hbm.1, bf16[2000,8192]{1,0:T(8,128)(2,1)} %bitcast.5, f32[1,1024]{1,0:T(1,128)} %bitcast.6, s32[1,1024]{1,0:T(1,128)} %bitcast.7), custom_call_target="tpu_custom_call" | custom-call | tf_op jit(solution)/shard_map/head/pallas_call | solution.py:290
  53.7 4.2 %write.1 = (f32[2000,1024]{1,0:T(8,128)}, f32[8,128]{1,0:T(8,128)}) custom-call(f32[8,2000,128]{2,1,0:T(8,128)S(1)} %get-tuple-element.8.sums_ref, f32[5,8,8,128]{3,2,1,0:T(8,128)S(1)} %get-tuple-element.9.gain_ref, f32[5,8,8,128]{3,2,1,0:T(8,128)S(1)} %get-tuple-element.10.off_ref, f32[8,128]{1,0:T(8,128)S(1)} %get-tuple-element.11.tsum_ref), custom_call_target="tpu_custom_call" | custom-call | tf_op jit(solution)/shard_map/write/pallas_call | solution.py:320

commit v5 on v4

--- a/solution.py
+++ b/solution.py
@@ -256,7 +256,7 @@
     ready = WIDE // LANES
     for block in range(n_block):
         for g in range(ready):
-            out_copy(block, g, sums_ref).start()
+            out_copy(block, g, sums_ref).start(priority=g % 2)
     for block in range(n_block):
         for g in range(ready, groups):
             gain = gain_ref[block, g]
@@ -264,7 +264,7 @@
             for i in range(STRIP):
                 rows = pl.ds(block * BLOCK + i, SUB, stride=STRIP)
                 stage[g - ready, rows, :] = sums_ref[g, rows, :] * gain + off
-            out_copy(block, g, stage, g - ready).start()
+            out_copy(block, g, stage, g - ready).start(priority=g % 2)
     for block in range(n_block):
         for g in range(groups):
             if g < ready:

time: 58.1 us -> 58.1 us (level)
  no operation moved by 1% of the time
where the time goes in v5:
time: 58.1 us; the launch traced here: 58 us
  Pallas kernels  57.2 us (98%)
  between operations  0.82 us (1%)
    pallas_call x1, Pallas kernels, local_fn(): pl.pallas_call(functools.partial(head_kernel, n_dev), out_shape=(jax.Shap...  53 us
    pallas_call x1, Pallas kernels, local_fn(): pl.pallas_call(write_kernel, out_shape=(jax.ShapeDtypeStruct((width, rows...  4.16 us

profile of v5, /device:TPU:21, one launch (start us, length us, event | category | flops | bytes accessed | tf_op | source)
XLA Modules:
  0.0 58.0 jit_solution(12390558170337634556)
XLA Ops:
  0.6 53.0 %head.1 = (f32[8,2000,128]{2,1,0:T(8,128)S(1)}, f32[5,8,8,128]{3,2,1,0:T(8,128)S(1)}, f32[5,8,8,128]{3,2,1,0:T(8,128)S(1)}, f32[8,128]{1,0:T(8,128)S(1)}) custom-call(bf16[1024,8192]{1,0:T(8,128)(2,1)} %h_hbm.1, bf16[2000,8192]{1,0:T(8,128)(2,1)} %bitcast.5, f32[1,1024]{1,0:T(1,128)} %bitcast.6, s32[1,1024]{1,0:T(1,128)} %bitcast.7), custom_call_target="tpu_custom_call" | custom-call | tf_op jit(solution)/shard_map/head/pallas_call | solution.py:290
  53.7 4.2 %write.1 = (f32[2000,1024]{1,0:T(8,128)}, f32[8,128]{1,0:T(8,128)}) custom-call(f32[8,2000,128]{2,1,0:T(8,128)S(1)} %get-tuple-element.8.sums_ref, f32[5,8,8,128]{3,2,1,0:T(8,128)S(1)} %get-tuple-element.9.gain_ref, f32[5,8,8,128]{3,2,1,0:T(8,128)S(1)} %get-tuple-element.10.off_ref, f32[8,128]{1,0:T(8,128)S(1)} %get-tuple-element.11.tsum_ref), custom_call_target="tpu_custom_call" | custom-call | tf_op jit(solution)/shard_map/write/pallas_call | solution.py:320
